TPU v7x, 32 devices: a whole 2x2x4 slice. The times are simulated.
32 devices in a mesh: row: 2 (over x), col: 16 (over z, y, core).
Axes of the slice: x: 2, y: 2, z: 4, core: 2. Of those that a mesh axis runs over, the one named last changes fastest.
Arguments:
- panel: bfloat16 [49152, 1024], P('col', 'row'), may hold values from -0.1875 to 0.1875
- rhs: float32 [1024, 49152], P('row', 'col'), may hold values from -6 to 6
- diag_inverse: bfloat16 [2, 512, 512], replicated, may hold values from -1 to 2, as said below
Outputs:
- solved: bfloat16 [1024, 1024], P(None, 'row')
- updated: float32 [1024, 49152], P('row', 'col')
Inputs may be any that keep to these rules, and one draw needn't show every extreme that they name: `diag_inverse`: each block is lower triangular; its diagonal entries are 0.5 or more.
All inputs are finite; a program needn't handle non-finite values.
Results may differ from a plain program's by a relative error of at most 0.0065.
Values may be sent and summed in bfloat16 or wider, within the bound.
A program may use at most 128 MiB of HBM per device.

v0:
```python
import jax
import jax.numpy as jnp
from jax import lax
from jax.sharding import PartitionSpec as P


def spread(value, axis, root):
    mine = lax.axis_index(axis) == root
    return lax.psum(jnp.where(mine, value, jnp.zeros_like(value)), axis)


def spread_block(values, owner):
    return spread(values, "col", owner)


def shards(panel, rhs, diag_inverse):
    block_size = diag_inverse.shape[1]
    step_count = diag_inverse.shape[0]
    slice_count = rhs.shape[0]
    rhs_count = slice_count * lax.axis_size("row")
    row_index = lax.axis_index("row")
    col_index = lax.axis_index("col")
    dropped = (col_index < step_count) & (row_index >= col_index)
    top_block = jnp.where(dropped, jnp.zeros_like(panel[:block_size]), panel[:block_size])
    masked = jnp.concatenate([top_block, panel[block_size:]], axis=0)
    contract = (((1,), (1,)), ((), ()))
    own_solved = jnp.zeros((rhs_count, block_size), jnp.bfloat16)
    for current in range(step_count):
        inverse = diag_inverse[current].astype(jnp.float32)
        partial_value = lax.cond(
            col_index == current,
            lambda: lax.dot_general(
                own_solved, masked[:block_size], contract, preferred_element_type=jnp.float32
            ),
            lambda: jnp.zeros((rhs_count, block_size), jnp.float32),
        )
        shares = lax.psum_scatter(partial_value, "row", scatter_dimension=0, tiled=True)
        residual = rhs[:, :block_size] - shares
        solution = jnp.dot(residual, inverse.T, precision=lax.Precision.HIGHEST).astype(
            jnp.bfloat16
        )
        share_arrived = spread_block(solution, current)
        arrived = lax.all_gather(share_arrived, "row", axis=0, tiled=True)
        own_solved = jnp.where(row_index == current, arrived, own_solved)
    reduced = lax.psum_scatter(
        lax.dot_general(own_solved, masked, contract, preferred_element_type=jnp.float32).astype(
            jnp.bfloat16
        ),
        "row",
        scatter_dimension=0,
        tiled=True,
    ).astype(jnp.float32)
    updated = rhs - reduced
    return (own_solved, updated)


def solution(mesh):
    placed = (P("col", "row"), P("row", "col"), P())
    return jax.shard_map(
        shards,
        mesh=mesh,
        in_specs=placed,
        out_specs=(P(None, "row"), P("row", "col")),
        check_vma=False,
    )
```

profile of v0, /device:TPU:0, one launch (start us, length us, event | category | flops | bytes accessed | tf_op | source)
XLA Modules:
  0.0 416.3 jit_solution(9032343016565336060)
XLA Ops:
  7.2 0.0 reduce-scatter.4.cloned.1.call-start
  7.2 1.1 slice_select_fusion
  8.3 0.8 conditional.2
  8.3 0.7 fusion
  9.1 0.0 copy-start
  9.1 1.3 copy-done
  10.4 0.0 reduce-scatter.4.cloned.1.call-update
  10.4 0.0 all-reduce.3.cloned.1.call-start
  10.5 35.0 %reduce-scatter.4.cloned.1.call-done = f32[512,512]{1,0:T(8,128)} async-done(((f32[1024,512]{1,0:T(8,128)}), f32[512,512]{1,0:T(8,128)}) %reduce-scatter.4.cloned.1.call-update) | async-done | bytes 1048592 | tf_op jit(solution)/shard_map/reduce_scatter | solution.py:37
  45.4 3.5 fusion.6
  48.9 0.0 all-reduce.3.cloned.1.call-update
  49.0 0.0 all-gather.3.cloned.1.call-start
  49.0 91.2 %all-reduce.3.cloned.1.call-done = bf16[512,512]{1,0:T(8,128)(2,1)} async-done(((bf16[512,512]{1,0:T(8,128)(2,1)}), bf16[512,512]{1,0:T(8,128)(2,1)}) %all-reduce.3.cloned.1.call-update) | async-done | bytes 524304 | tf_op jit(solution)/shard_map/psum | solution.py:9
  140.2 0.0 all-gather.3.cloned.1.call-update
  140.2 0.0 reduce-scatter.6.cloned.1.call-start
  140.2 23.2 %all-gather.3.cloned.1.call-done = bf16[1024,512]{1,0:T(8,128)(2,1)} async-done(((bf16[512,512]{1,0:T(8,128)(2,1)}), bf16[1024,512]{1,0:T(8,128)(2,1)}) %all-gather.3.cloned.1.call-update) | async-done | bytes 1048592 | tf_op jit(solution)/shard_map/all_gather | solution.py:43
  163.5 1.3 broadcast_select_fusion
  164.8 0.3 conditional.3
  164.8 0.2 broadcast.7
  165.1 0.0 copy-start.1
  165.1 1.3 copy-done.1
  166.4 0.0 reduce-scatter.6.cloned.1.call-update
  166.4 0.0 all-reduce.5.cloned.1.call-start
  166.5 32.0 %reduce-scatter.6.cloned.1.call-done = f32[512,512]{1,0:T(8,128)} async-done(((f32[1024,512]{1,0:T(8,128)}), f32[512,512]{1,0:T(8,128)}) %reduce-scatter.6.cloned.1.call-update) | async-done | bytes 1048592 | tf_op jit(solution)/shard_map/reduce_scatter | solution.py:37
  198.5 3.5 fusion.7
  202.0 0.0 copy-start.2
  202.0 0.0 all-reduce.5.cloned.1.call-update
  202.0 0.0 all-gather.5.cloned.1.call-start
  202.0 91.0 %all-reduce.5.cloned.1.call-done = bf16[512,512]{1,0:T(8,128)(2,1)} async-done(((bf16[512,512]{1,0:T(8,128)(2,1)}), bf16[512,512]{1,0:T(8,128)(2,1)}) %all-reduce.5.cloned.1.call-update) | async-done | bytes 524304 | tf_op jit(solution)/shard_map/psum | solution.py:9
  293.0 0.0 all-gather.5.cloned.1.call-update
  293.1 0.0 reduce-scatter.8.cloned.1.call-start
  293.1 23.1 %all-gather.5.cloned.1.call-done = bf16[1024,512]{1,0:T(8,128)(2,1)} async-done(((bf16[512,512]{1,0:T(8,128)(2,1)}), bf16[1024,512]{1,0:T(8,128)(2,1)}) %all-gather.5.cloned.1.call-update) | async-done | bytes 1048592 | tf_op jit(solution)/shard_map/all_gather | solution.py:43
  316.2 0.0 copy-done.2
  316.2 0.0 slice-start
  316.2 0.1 broadcast_select_fusion.1
  316.3 1.6 slice-done
  317.9 0.0 copy-start.3
  317.9 6.2 %convolution_convert_fusion = bf16[1024,3072]{1,0:T(8,128)(2,1)} fusion(bf16[1024,512]{1,0:T(8,128)(2,1)S(1)} %broadcast_select_fusion.1, bf16[2560,512]{1,0:T(8,128)(2,1)S(1)} %slice-done, bf16[512,512]{1,0:T(8,128)(2,1)S(1)} %slice_select_fusion), kind=kOutput, calls=%fused_computation.4 | convolution fusion | flops 3230662656 | bytes 10485760 | tf_op jit(solution)/shard_map/dot_general | solution.py:46
  324.1 0.0 copy-done.3
  324.1 0.0 reduce-scatter.8.cloned.1.call-update
  324.2 77.6 %reduce-scatter.8.cloned.1.call-done = bf16[512,3072]{1,0:T(8,128)(2,1)} async-done(((bf16[1024,3072]{1,0:T(8,128)(2,1)}), bf16[512,3072]{1,0:T(8,128)(2,1)}) %reduce-scatter.8.cloned.1.call-update) | async-done | bytes 3145744 | tf_op jit(solution)/shard_map/reduce_scatter | solution.py:45
  401.8 7.7 %convert_subtract_fusion = f32[512,3072]{1,0:T(8,128)} fusion(f32[512,3072]{1,0:T(8,128)} %param.8, bf16[512,3072]{1,0:T(8,128)(2,1)} %reduce-scatter.8.cloned.1.call-done), kind=kLoop, calls=%fused_computation.3 | loop fusion | flops 3145728 | bytes 15728640 | tf_op jit(solution)/shard_map/sub | solution.py:53
Async XLA Ops:
  7.2 38.3 %reduce-scatter.4.cloned.1.call-start = ((), (), s32[]{:S(2)}) async-start(), calls=%async_computation.3 | async-start | bytes 3145728 | tf_op jit(solution)/shard_map/reduce_scatter | solution.py:37
  9.1 1.3 copy-start
  10.4 129.7 %all-reduce.3.cloned.1.call-start = ((), (), s32[]{:S(2)}) async-start(), calls=%async_computation.4 | async-start | bytes 1048576 | tf_op jit(solution)/shard_map/psum | solution.py:9
  49.0 114.5 %all-gather.3.cloned.1.call-start = ((), (), s32[]{:S(2)}) async-start(), calls=%async_computation.5 | async-start | bytes 1572864 | tf_op jit(solution)/shard_map/all_gather | solution.py:43
  140.2 58.3 %reduce-scatter.6.cloned.1.call-start = ((), (), s32[]{:S(2)}) async-start(), calls=%async_computation.6 | async-start | bytes 3145728 | tf_op jit(solution)/shard_map/reduce_scatter | solution.py:37
  165.1 1.3 copy-start.1
  166.4 126.6 %all-reduce.5.cloned.1.call-start = ((), (), s32[]{:S(2)}) async-start(), calls=%async_computation.7 | async-start | bytes 1048576 | tf_op jit(solution)/shard_map/psum | solution.py:9
  202.0 114.2 %copy-start.2 = (bf16[1024,512]{1,0:T(8,128)(2,1)S(1)}, bf16[1024,512]{1,0:T(8,128)(2,1)}, u32[]{:S(2)}) copy-start(bf16[1024,512]{1,0:T(8,128)(2,1)} %all-gather.3.cloned.1.call-done) | copy-start | bytes 3145732
  202.0 114.2 %all-gather.5.cloned.1.call-start = ((), (), s32[]{:S(2)}) async-start(), calls=%async_computation.8 | async-start | bytes 1572864 | tf_op jit(solution)/shard_map/all_gather | solution.py:43
  293.1 108.7 %reduce-scatter.8.cloned.1.call-start = ((), (), s32[]{:S(2)}) async-start(), calls=%async_computation.9 | async-start | bytes 9437184 | tf_op jit(solution)/shard_map/reduce_scatter | solution.py:45
  316.2 1.7 slice-start
  317.9 6.2 %copy-start.3 = (bf16[1024,512]{1,0:T(8,128)(2,1)}, bf16[1024,512]{1,0:T(8,128)(2,1)S(1)}, u32[]{:S(2)}) copy-start(bf16[1024,512]{1,0:T(8,128)(2,1)S(1)} %broadcast_select_fusion.1) | copy-start | bytes 3145732
Sparse Core Ops, SparseCore 0:
  10.8 34.6 reduce-scatter.3
  49.4 90.7 all-reduce.2
  141.7 21.7 all-gather.2
  166.5 31.8 reduce-scatter.5
  202.3 90.6 all-reduce.4
  294.4 21.7 all-gather.4
  324.3 77.4 reduce-scatter.7
where the time goes:
time: 417 us; the launch traced here: 416 us
  waiting for transfers between devices  373 us (89%)
  between operations  14.2 us (3%)
  matrix products  13.9 us (3%)
  other arithmetic  10.2 us (2%)
  local copies, waits for them, and re-layouts  4.51 us (1%)
    psum x2, waiting for transfers between devices, spread(): return lax.psum(jnp.where(mine, value, jnp.zeros_like(value)), axis)  182 us
    reduce_scatter x1, waiting for transfers between devices, shards(): lax.psum_scatter(lax.dot_general(own_solved, masked, contract, preferred_...  77.6 us
    reduce_scatter x2, waiting for transfers between devices, shards(): lax.psum_scatter(partial_value, 'row', scatter_dimension=0, tiled=True)  67 us
    all_gather x2, waiting for transfers between devices, shards(): arrived = lax.all_gather(share_arrived, 'row', axis=0, tiled=True)  46.3 us
  transfers between devices with their start and end apart: 7, of which 7 were waited for; matrix products, arithmetic and copies ran while one was open for 0% of the time, Pallas kernels for 0%

commit v1 on v0

--- a/solution.py
+++ b/solution.py
@@ -6,7 +6,7 @@
 
 def spread(value, axis, root):
     mine = lax.axis_index(axis) == root
-    return lax.psum(jnp.where(mine, value, jnp.zeros_like(value)), axis)
+    return jnp.sum(lax.all_gather(jnp.where(mine, value, jnp.zeros_like(value)), axis), axis=0)
 
 
 def spread_block(values, owner):

time: 417 us -> 388 us (0.930)
  waiting for transfers between devices: 373 us -> 333 us
  other arithmetic: 10.2 us -> 21.2 us
    psum x2 -> x0, waiting for transfers between devices: 182 us -> none  [spread(): return lax.psum(jnp.where(mine, value, jnp.zeros_like(value)), axis)]
    all_gather x0 -> x2, waiting for transfers between devices: none -> 149 us  [spread(): lax.all_gather(jnp.where(mine, value, jnp.zeros_like(value)), axis)]
    reduce_sum x0 -> x2, other arithmetic: none -> 11 us  [spread(): jnp.sum(lax.all_gather(jnp.where(mine, value, jnp.zeros_like(value)), axi...]
    all_gather x2, waiting for transfers between devices: 46.3 us -> 39.9 us  [shards(): arrived = lax.all_gather(share_arrived, 'row', axis=0, tiled=True)]
where the time goes in v1:
time: 388 us
  waiting for transfers between devices  333 us (86%)
  other arithmetic  21.2 us (5%)
  between operations  14.2 us (4%)
  matrix products  13.9 us (4%)
  local copies, waits for them, and re-layouts  4.51 us (1%)
    all_gather x2, waiting for transfers between devices, spread(): lax.all_gather(jnp.where(mine, value, jnp.zeros_like(value)), axis)  149 us
    reduce_scatter x1, waiting for transfers between devices, shards(): lax.psum_scatter(lax.dot_general(own_solved, masked, contract, preferred_...  77.6 us
    reduce_scatter x2, waiting for transfers between devices, shards(): lax.psum_scatter(partial_value, 'row', scatter_dimension=0, tiled=True)  67 us
    all_gather x2, waiting for transfers between devices, shards(): arrived = lax.all_gather(share_arrived, 'row', axis=0, tiled=True)  39.9 us
    reduce_sum x2, other arithmetic, spread(): jnp.sum(lax.all_gather(jnp.where(mine, value, jnp.zeros_like(value)), axi...  11 us
  transfers between devices with their start and end apart: 7, of which 7 were waited for; matrix products, arithmetic and copies ran while one was open for 0% of the time, Pallas kernels for 0%

profile of v1, /device:TPU:0, one launch (start us, length us, event | category | flops | bytes accessed | tf_op | source)
XLA Modules:
  0.0 387.6 jit_solution(4364125449873139194)
XLA Ops:
  7.2 0.0 reduce-scatter.4.cloned.1.call-start
  7.2 1.1 slice_select_fusion
  8.3 0.8 conditional.2
  8.3 0.7 fusion
  9.1 0.0 copy-start
  9.1 1.3 copy-done
  10.4 0.0 reduce-scatter.4.cloned.1.call-update
  10.4 0.0 all-gather.11.cloned.1.call-start
  10.5 35.0 %reduce-scatter.4.cloned.1.call-done = f32[512,512]{1,0:T(8,128)} async-done(((f32[1024,512]{1,0:T(8,128)}), f32[512,512]{1,0:T(8,128)}) %reduce-scatter.4.cloned.1.call-update) | async-done | bytes 1048592 | tf_op jit(solution)/shard_map/reduce_scatter | solution.py:37
  45.4 3.5 fusion.6
  48.9 0.0 all-gather.11.cloned.1.call-update
  49.0 0.0 all-gather.7.cloned.1.call-start
  49.0 74.4 %all-gather.11.cloned.1.call-done = bf16[8192,512]{1,0:T(8,128)(2,1)} async-done(((bf16[512,512]{1,0:T(8,128)(2,1)}), bf16[8192,512]{1,0:T(8,128)(2,1)}) %all-gather.11.cloned.1.call-update) | async-done | bytes 8388624 | tf_op jit(solution)/shard_map/all_gather | solution.py:9
  123.4 5.5 %reduce_sum.24 = bf16[512,512]{1,0:T(8,128)(2,1)} reduce(bf16[16,512,512]{2,1,0:T(8,128)(2,1)} %bitcast.13, bf16[]{:T(256)} %constant.26.clone.1), dimensions={0}, to_apply=%region_3.4 | reduce | flops 3932160 | bytes 8912898 | tf_op jit(solution)/shard_map/reduce_sum | solution.py:9
  128.9 0.0 all-gather.7.cloned.1.call-update
  128.9 0.0 reduce-scatter.6.cloned.1.call-start
  129.0 20.0 %all-gather.7.cloned.1.call-done = bf16[1024,512]{1,0:T(8,128)(2,1)} async-done(((bf16[512,512]{1,0:T(8,128)(2,1)}), bf16[1024,512]{1,0:T(8,128)(2,1)}) %all-gather.7.cloned.1.call-update) | async-done | bytes 1048592 | tf_op jit(solution)/shard_map/all_gather | solution.py:43
  149.0 1.3 broadcast_select_fusion
  150.3 0.3 conditional.3
  150.3 0.2 broadcast.7
  150.5 0.0 copy-start.1
  150.6 1.3 copy-done.1
  151.9 0.0 reduce-scatter.6.cloned.1.call-update
  151.9 0.0 all-gather.13.cloned.1.call-start
  151.9 32.0 %reduce-scatter.6.cloned.1.call-done = f32[512,512]{1,0:T(8,128)} async-done(((f32[1024,512]{1,0:T(8,128)}), f32[512,512]{1,0:T(8,128)}) %reduce-scatter.6.cloned.1.call-update) | async-done | bytes 1048592 | tf_op jit(solution)/shard_map/reduce_scatter | solution.py:37
  184.0 3.5 fusion.7
  187.4 0.0 all-gather.13.cloned.1.call-update
  187.5 0.0 all-gather.9.cloned.1.call-start
  187.5 74.4 %all-gather.13.cloned.1.call-done = bf16[8192,512]{1,0:T(8,128)(2,1)} async-done(((bf16[512,512]{1,0:T(8,128)(2,1)}), bf16[8192,512]{1,0:T(8,128)(2,1)}) %all-gather.13.cloned.1.call-update) | async-done | bytes 8388624 | tf_op jit(solution)/shard_map/all_gather | solution.py:9
  261.9 5.5 %reduce_sum.25 = bf16[512,512]{1,0:T(8,128)(2,1)} reduce(bf16[16,512,512]{2,1,0:T(8,128)(2,1)} %bitcast.12, bf16[]{:T(256)} %constant.26.clone.1), dimensions={0}, to_apply=%region_7.8 | reduce | flops 3932160 | bytes 8912898 | tf_op jit(solution)/shard_map/reduce_sum | solution.py:9
  267.4 0.0 copy-start.2
  267.4 0.0 all-gather.9.cloned.1.call-update
  267.4 0.0 reduce-scatter.8.cloned.1.call-start
  267.5 20.0 %all-gather.9.cloned.1.call-done = bf16[1024,512]{1,0:T(8,128)(2,1)} async-done(((bf16[512,512]{1,0:T(8,128)(2,1)}), bf16[1024,512]{1,0:T(8,128)(2,1)}) %all-gather.9.cloned.1.call-update) | async-done | bytes 1048592 | tf_op jit(solution)/shard_map/all_gather | solution.py:43
  287.5 0.0 copy-done.2
  287.5 0.0 slice-start
  287.5 0.1 broadcast_select_fusion.1
  287.6 1.6 slice-done
  289.2 0.0 copy-start.3
  289.2 6.2 %convolution_convert_fusion = bf16[1024,3072]{1,0:T(8,128)(2,1)} fusion(bf16[1024,512]{1,0:T(8,128)(2,1)S(1)} %broadcast_select_fusion.1, bf16[2560,512]{1,0:T(8,128)(2,1)S(1)} %slice-done, bf16[512,512]{1,0:T(8,128)(2,1)S(1)} %slice_select_fusion), kind=kOutput, calls=%fused_computation.4 | convolution fusion | flops 3230662656 | bytes 10485760 | tf_op jit(solution)/shard_map/dot_general | solution.py:46
  295.4 0.0 copy-done.3
  295.4 0.0 reduce-scatter.8.cloned.1.call-update
  295.4 77.6 %reduce-scatter.8.cloned.1.call-done = bf16[512,3072]{1,0:T(8,128)(2,1)} async-done(((bf16[1024,3072]{1,0:T(8,128)(2,1)}), bf16[512,3072]{1,0:T(8,128)(2,1)}) %reduce-scatter.8.cloned.1.call-update) | async-done | bytes 3145744 | tf_op jit(solution)/shard_map/reduce_scatter | solution.py:45
  373.0 7.7 %convert_subtract_fusion = f32[512,3072]{1,0:T(8,128)} fusion(f32[512,3072]{1,0:T(8,128)} %param.8, bf16[512,3072]{1,0:T(8,128)(2,1)} %reduce-scatter.8.cloned.1.call-done), kind=kLoop, calls=%fused_computation.3 | loop fusion | flops 3145728 | bytes 15728640 | tf_op jit(solution)/shard_map/sub | solution.py:53
Async XLA Ops:
  7.2 38.3 %reduce-scatter.4.cloned.1.call-start = ((), (), s32[]{:S(2)}) async-start(), calls=%async_computation.3 | async-start | bytes 3145728 | tf_op jit(solution)/shard_map/reduce_scatter | solution.py:37
  9.1 1.3 copy-start
  10.4 113.0 %all-gather.11.cloned.1.call-start = ((), (), s32[]{:S(2)}) async-start(), calls=%async_computation.8 | async-start | bytes 8912896 | tf_op jit(solution)/shard_map/all_gather | solution.py:9
  49.0 100.0 %all-gather.7.cloned.1.call-start = ((), (), s32[]{:S(2)}) async-start(), calls=%async_computation.4 | async-start | bytes 1572864 | tf_op jit(solution)/shard_map/all_gather | solution.py:43
  128.9 55.0 %reduce-scatter.6.cloned.1.call-start = ((), (), s32[]{:S(2)}) async-start(), calls=%async_computation.5 | async-start | bytes 3145728 | tf_op jit(solution)/shard_map/reduce_scatter | solution.py:37
  150.5 1.3 copy-start.1
  151.9 110.0 %all-gather.13.cloned.1.call-start = ((), (), s32[]{:S(2)}) async-start(), calls=%async_computation.9 | async-start | bytes 8912896 | tf_op jit(solution)/shard_map/all_gather | solution.py:9
  187.5 100.0 %all-gather.9.cloned.1.call-start = ((), (), s32[]{:S(2)}) async-start(), calls=%async_computation.6 | async-start | bytes 1572864 | tf_op jit(solution)/shard_map/all_gather | solution.py:43
  267.4 20.0 %copy-start.2 = (bf16[1024,512]{1,0:T(8,128)(2,1)S(1)}, bf16[1024,512]{1,0:T(8,128)(2,1)}, u32[]{:S(2)}) copy-start(bf16[1024,512]{1,0:T(8,128)(2,1)} %all-gather.7.cloned.1.call-done) | copy-start | bytes 3145732
  267.4 105.6 %reduce-scatter.8.cloned.1.call-start = ((), (), s32[]{:S(2)}) async-start(), calls=%async_computation.7 | async-start | bytes 9437184 | tf_op jit(solution)/shard_map/reduce_scatter | solution.py:45
  287.5 1.7 slice-start
  289.2 6.2 %copy-start.3 = (bf16[1024,512]{1,0:T(8,128)(2,1)}, bf16[1024,512]{1,0:T(8,128)(2,1)S(1)}, u32[]{:S(2)}) copy-start(bf16[1024,512]{1,0:T(8,128)(2,1)S(1)} %broadcast_select_fusion.1) | copy-start | bytes 3145732
Sparse Core Ops, SparseCore 0:
  10.8 34.6 reduce-scatter.3
  49.1 74.2 all-gather.10
  129.1 19.8 all-gather.6
  152.0 31.8 reduce-scatter.5
  187.6 74.2 all-gather.12
  267.6 19.8 all-gather.8
  295.5 77.4 reduce-scatter.7
